TPU v7x, 256 devices: a whole 4x4x8 slice. The times are simulated.
256 devices in a mesh: wa: 64 (over x_hi, y, z), ba: 4 (over x_lo, core).
Axes of the slice: x: 4 (x_hi: 2, x_lo: 2; x = x_hi * 2 + x_lo), y: 4, z: 8, core: 2. Of those that a mesh axis runs over, the one named last changes fastest.
Arguments:
- latent: float32 [16, 8, 8192], P('ba', None, 'wa'), parts along dimension 0, may hold values from -12 to 12
- noise: float32 [2, 16, 8, 8192], P(None, 'ba', None, 'wa'), parts along dimension 1, may hold values from -6 to 6
- offsets: int32 [128], P('wa'), may hold values from 0 to 63
- anchors: int32 [2], replicated, may hold values from 0 to 127
- guidance: float32 [1], replicated, may hold values from 0.4 to 0.8
- w_in: bfloat16 [320, 36], replicated, may hold values from -1 to 1
- w_mid: bfloat16 [320, 320], replicated, may hold values from -0.3125 to 0.3125
- w_out: bfloat16 [36, 320], replicated, may hold values from -0.109375 to 0.109375
- t_embed: float32 [2, 320], replicated, may hold values from -6 to 6
- w_feat: float32 [64, 4], replicated, may hold values from -3 to 3
Outputs:
- denoised: float32 [16, 8, 8192], P('ba', None, 'wa'), parts along dimension 0
There are 4 independent parts, one for each index of `ba`. A program takes and returns all parts, laid end to end along the dimension named above; an argument that names none is the same for every part. Nothing has to cross between parts.
All inputs are finite; a program needn't handle non-finite values.
Results may differ from a plain program's by a relative error of at most 0.0065.
Values sent between devices are 32-bit elements; how exact they have to be, the bound alone decides.
No kernel may reach another device: no remote copies, remote signals or barrier semaphores. Data moves between devices by JAX's collectives and lax.ppermute only.
A program may use at most 64 MiB of HBM per device.

v0:
```python
import math
import jax
import jax.numpy as jnp
from jax import lax
from jax.sharding import Mesh
from jax.sharding import PartitionSpec as P

WIN = 128
STRIDE = 64
STEPS = 2
WA = ("wa_0", "wa_1", "wa_2")
TAP_SHIFTS = ((-1, -1), (-1, 0), (-1, 1), (0, -1), (0, 0), (0, 1), (1, -1), (1, 0), (1, 1))
CUMULATIVE_ALPHA = (0.35, 0.55, 0.72, 0.85, 0.93)
STABILITY = 1e-06


def broadcast_by_axis(shard, axes, root):
    shard = jnp.where(lax.axis_index(axes) == root, shard, jnp.zeros_like(shard))
    for axis in axes:
        shard = lax.psum(shard, axis)
    return shard


def from_everyone(shard, axis):
    copies = jnp.broadcast_to(shard, (lax.axis_size(axis), *shard.shape))
    return lax.all_to_all(copies, axis, split_axis=0, concat_axis=0, tiled=True)


def of_everyone(shard, axis):
    return from_everyone(shard, axis).sum(axis=0)


def passed_along(shard, axis, by):
    length = lax.axis_size(axis)
    return lax.ppermute(shard, axis, [(i, (i + by) % length) for i in range(length)])


def plan(number):
    current = CUMULATIVE_ALPHA[number]
    following = CUMULATIVE_ALPHA[number + 1]
    spread = 0.3 * math.sqrt(1.0 - following)
    return (
        math.sqrt(current),
        math.sqrt(1.0 - current),
        math.sqrt(following),
        math.sqrt(1.0 - following - spread * spread),
        spread,
    )


def tapped(field):
    height, columns = (field.shape[-2], field.shape[-1])
    padding = [(0, 0)] * (field.ndim - 2) + [(1, 1), (1, 1)]
    padded = jnp.pad(field, padding)
    return jnp.stack(
        [
            padded[..., 1 + down_by : 1 + down_by + height, 1 + right_by : 1 + right_by + columns]
            for down_by, right_by in TAP_SHIFTS
        ]
    )


def denoise(window, w_in, w_mid, w_out, embedding):
    channels, height, columns = window.shape
    stacked = tapped(window.astype(jnp.bfloat16)).reshape(9 * channels, height * columns)
    hidden_in = jnp.dot(w_in, stacked, preferred_element_type=jnp.float32) + embedding[:, None]
    activated = jax.nn.silu(hidden_in).astype(jnp.bfloat16)
    middle = jnp.dot(w_mid, activated, preferred_element_type=jnp.float32)
    joined = (hidden_in + jax.nn.silu(middle)).astype(jnp.bfloat16)
    outward = jnp.dot(w_out, joined, preferred_element_type=jnp.float32).reshape(
        9, channels, height, columns
    )
    padded = jnp.pad(outward, ((0, 0), (0, 0), (1, 1), (1, 1)))
    result = jnp.zeros((channels, height, columns), jnp.float32)
    for index, (down_by, right_by) in enumerate(TAP_SHIFTS):
        result = (
            result
            + padded[
                index, :, 1 + down_by : 1 + down_by + height, 1 + right_by : 1 + right_by + columns
            ]
        )
    return result


def clean_of(windows, w_in, w_mid, w_out, embedding, now_a, now_s):
    predicted = jax.vmap(denoise, (0, None, None, None, None))(
        windows, w_in, w_mid, w_out, embedding
    )
    cleaned = (windows - now_s * predicted) / now_a
    return (cleaned, predicted)


def percept(cleaned, w_feat):
    return jax.nn.silu(jnp.einsum("fc,chw->fhw", w_feat, cleaned, precision=lax.Precision.HIGHEST))


def mismatch(cleaned, anchor_percept, w_feat):
    difference = percept(cleaned, w_feat) - anchor_percept
    return 0.5 * jnp.sum(difference * difference) / w_feat.shape[0]


def finish_gradient(cleaned, pullback, anchor_percept, w_feat):
    clean_grad = jax.vmap(jax.grad(mismatch), (0, None, None))(cleaned, anchor_percept, w_feat)
    return pullback(clean_grad)[0]


def advance(windows, gradient, predicted, scale, now_a, now_s, next_a, direction):
    return next_a * (windows - scale * gradient - now_s * predicted) / now_a + direction * predicted


def window_update(extended, number, starts, anchors, guidance, w_in, w_mid, w_out, t_embed, w_feat):
    per_dev = starts.shape[0]
    now_a, now_s, next_a, direction, spread = plan(number)
    embedding = t_embed[number]
    windows = jnp.stack(
        [lax.dynamic_slice_in_dim(extended, starts[index], WIN, 2) for index in range(per_dev)]
    )

    def cleaning(inputs):
        return clean_of(inputs, w_in, w_mid, w_out, embedding, now_a, now_s)

    cleaned, pullback, predicted = jax.vjp(cleaning, windows, has_aux=True)
    owner = anchors[number] // per_dev
    slot = anchors[number] % per_dev
    picked = lax.dynamic_index_in_dim(cleaned, slot, 0, keepdims=False)
    anchor_percept = percept(broadcast_by_axis(picked, WA, owner), w_feat)
    gradient = finish_gradient(cleaned, pullback, anchor_percept, w_feat)
    square_sum = of_everyone(jnp.sum(gradient * gradient), WA)
    element_count = per_dev * lax.axis_size(WA) * windows.shape[1] * windows.shape[2] * WIN
    scale = guidance[0] * lax.rsqrt(square_sum / element_count + STABILITY)
    advanced = advance(windows, gradient, predicted, scale, now_a, now_s, next_a, direction)
    summed = jnp.zeros(extended.shape, jnp.float32)
    for index in range(per_dev):
        current = lax.dynamic_slice_in_dim(summed, starts[index], WIN, 2)
        summed = lax.dynamic_update_slice_in_dim(
            summed, current + advanced[index], starts[index], 2
        )
    return (summed, spread)


def local(latent, noise, offsets, anchors, guidance, w_in, w_mid, w_out, t_embed, w_feat):
    width = latent.shape[-1]
    per_dev = offsets.shape[0]
    starts = jnp.arange(per_dev, dtype=jnp.int32) * STRIDE + offsets
    positions = jnp.arange(2 * width, dtype=jnp.int32)
    inside = (positions[None, :] >= starts[:, None]) & (positions[None, :] < starts[:, None] + WIN)
    cover = jnp.sum(inside.astype(jnp.float32), axis=0)
    count_own = cover[:width] + passed_along(cover[width:], WA, 1)
    state = latent
    for number in range(STEPS):
        neighbour = passed_along(state, WA, -1)
        extended = jnp.concatenate([state, neighbour], axis=2)
        summed, spread = window_update(
            extended, number, starts, anchors, guidance, w_in, w_mid, w_out, t_embed, w_feat
        )
        spill = passed_along(summed[:, :, width:], WA, 1)
        state = (summed[:, :, :width] + spill) / count_own + spread * noise[number]
    return state


def solution(mesh):
    finer = Mesh(mesh.devices.reshape(2, 4, 8, mesh.shape["ba"]), ("wa_0", "wa_1", "wa_2", "ba"))
    placed = (P("ba", None, WA), P(None, "ba", None, WA), P(WA), P(), P(), P(), P(), P(), P(), P())
    return jax.shard_map(
        local, mesh=finer, in_specs=placed, out_specs=P("ba", None, WA), check_vma=False
    )
```

profile of v0, /device:TPU:2, one launch (start us, length us, event | category | flops | bytes accessed | tf_op | source)
XLA Modules:
  0.0 238.8 jit_solution(6218011149825673397)
XLA Ops:
  0.0 0.8 fusion.239
  0.8 9.9 %collective-permute-start = (f32[4,8,128]{2,0,1:T(4,128)S(1)}, f32[4,8,128]{2,0,1:T(4,128)S(1)}, u32[]{:S(2)}, u32[]{:S(2)}) collective-permute-start(f32[4,8,128]{2,0,1:T(4,128)S(1)} %get-tuple-element.43), channel_id=1, source_target_pairs={{0,252},{4,0},{8,4},{12,8},{16,12},{20,16},{24,20},{28,24},{32,28}... | collective-permute-start | bytes 49160 | tf_op jit(solution)/shard_map/ppermute | solution.py:35
  10.6 0.7 broadcast_add_fusion
  12.0 0.6 fusion.241
  12.6 1.4 slice_reduce_fusion
  13.9 1.4 fusion.240
  22.8 1.3 fusion.190
  24.1 2.6 %fusion.88 = f32[2,1024,320]{1,2,0:T(8,128)} fusion(f32[2,1024,320]{1,2,0:T(8,128)S(1)} %fusion.190, f32[320]{0:T(512)S(1)} %get-tuple-element.6, bf16[320,320]{1,0:T(8,128)(2,1)S(1)} %copy-done), kind=kOutput, calls=%fused_computation.107 | convolution fusion | flops 423362560 | bytes 5448960 | tf_op jit(solution)/shard_map/jvp(vmap())/dot_general | solution.py:68
  26.7 2.6 %fusion.94 = f32[2,36,1024]{2,1,0:T(8,128)S(1)} fusion(f32[2,1024,320]{1,2,0:T(8,128)} %fusion.88, f32[2,1024,320]{1,2,0:T(8,128)S(1)} %fusion.190, f32[320]{0:T(512)S(1)} %get-tuple-element.6, bf16[36,320]{1,0:T(8,128)(2,1)S(1)} %copy-done.3), kind=kOutput, calls=%fused_computation.112 | convolution fusion | flops 51773440 | bytes 5562112 | tf_op jit(solution)/shard_map/jvp(vmap())/dot_general | solution.py:70
  29.7 9.6 %psum.42 = f32[4,8,128]{2,0,1:T(4,128)S(1)} all-reduce(f32[4,8,128]{2,0,1:T(4,128)S(1)} %select_bitcast_fusion.1), channel_id=1, replica_groups=mesh['wa_0'=2,'wa_1'=4,'wa_2'=8,'ba'=4] {'wa_0'}, use_global_device_ids=true, to_apply=%region_0.0 | all-reduce | flops 4096 | bytes 32768 | tf_op jit(solution)/shard_map/psum | solution.py:20
  39.2 14.3 %psum.43 = f32[4,8,128]{2,0,1:T(4,128)S(1)} all-reduce(f32[4,8,128]{2,0,1:T(4,128)S(1)} %psum.42), channel_id=1, replica_groups=mesh['wa_0'=2,'wa_1'=4,'wa_2'=8,'ba'=4] {'wa_1'}, use_global_device_ids=true, to_apply=%region_1.2 | all-reduce | flops 4096 | bytes 32768 | tf_op jit(solution)/shard_map/psum | solution.py:20
  53.5 34.2 %psum.44 = f32[4,8,128]{2,0,1:T(4,128)S(1)} all-reduce(f32[4,8,128]{2,0,1:T(4,128)S(1)} %psum.43), channel_id=1, replica_groups=mesh['wa_0'=2,'wa_1'=4,'wa_2'=8,'ba'=4] {'wa_2'}, use_global_device_ids=true, to_apply=%region_2.3 | all-reduce | flops 4096 | bytes 32768 | tf_op jit(solution)/shard_map/psum | solution.py:20
  87.7 1.3 convolution_bitcast_fusion.1
  89.0 1.1 divide_multiply_fusion.1
  90.2 0.6 fusion.121
  91.4 1.6 convolution_convert_fusion.1
  93.0 5.1 %fusion.110 = bf16[2,36,1024]{2,1,0:T(8,128)(2,1)S(1)} fusion(bf16[2,1024,320]{1,2,0:T(8,128)(2,1)} %convolution_convert_fusion.1, f32[2,1024,320]{1,2,0:T(8,128)S(1)} %fusion.190, f32[2,1024,320]{1,2,0:T(8,128)} %fusion.88, f32[320]{0:T(512)S(1)} %copy-done.13, bf16[320,320]{1,0:T(8,128)(2,1)S(1)} %copy-done, bf16[320,36]{0,1:T(8,128)(2,1)S(1)} %copy-done.1), kind=kOutput, calls=%fused_computation.118 | convolution fusion | flops 482418688 | bytes 6930176 | tf_op jit(solution)/shard_map/transpose(jvp(vmap()))/dot_general | solution.py:66
  98.5 0.7 multiply_reduce_fusion.1
  99.2 1.3 broadcast_in_dim.9
  100.4 4.8 %all-to-all-start = ((f32[64,1,1]{2,1,0:T(1,128)}), f32[64,1,1]{2,1,0:T(1,128)S(1)}, u32[]{:S(2)}, u32[]{:S(2)}) async-start(f32[64,1,1]{2,1,0:T(1,128)} %broadcast_in_dim.9), calls=%async_computation | async-start | bytes 65536 | tf_op jit(solution)/shard_map/all_to_all | solution.py:26
  105.2 0.6 slice_multiply_fusion.1
  106.5 10.6 %all-to-all-done = f32[64,1,1]{2,1,0:T(1,128)S(1)} async-done(((f32[64,1,1]{2,1,0:T(1,128)}), f32[64,1,1]{2,1,0:T(1,128)S(1)}, u32[]{:S(2)}, u32[]{:S(2)}) %all-to-all-start) | async-done | bytes 288 | tf_op jit(solution)/shard_map/all_to_all | solution.py:26
  117.1 0.7 reduce_sum.46
  118.5 1.3 dynamic_update_slice.12
  119.9 1.3 dynamic_update_slice.13
  121.2 0.7 collective-permute-start.1
  121.9 0.6 slice_add_fusion.2
  122.5 8.3 %collective-permute-done.1 = f32[4,8,128]{2,0,1:T(4,128)S(1)} collective-permute-done((f32[4,8,128]{2,0,1:T(4,128)S(1)}, f32[4,8,128]{2,0,1:T(4,128)S(1)}, u32[]{:S(2)}, u32[]{:S(2)}) %collective-permute-start.1) | collective-permute-done | bytes 16416 | tf_op jit(solution)/shard_map/ppermute | solution.py:35
  133.4 1.2 collective-permute-done.3
  136.2 1.1 fusion.86
  137.2 1.5 copy-done.16
  138.7 0.9 fusion.97
  140.0 1.3 convolution_bitcast_fusion
  141.3 8.9 %psum.45 = f32[4,8,128]{2,0,1:T(4,128)S(1)} all-reduce(f32[4,8,128]{2,0,1:T(4,128)S(1)} %select_bitcast_fusion), channel_id=1, replica_groups=mesh['wa_0'=2,'wa_1'=4,'wa_2'=8,'ba'=4] {'wa_0'}, use_global_device_ids=true, to_apply=%region_6.7 | all-reduce | flops 4096 | bytes 32768 | tf_op jit(solution)/shard_map/psum | solution.py:20
  150.2 14.3 %psum.46 = f32[4,8,128]{2,0,1:T(4,128)S(1)} all-reduce(f32[4,8,128]{2,0,1:T(4,128)S(1)} %psum.45), channel_id=1, replica_groups=mesh['wa_0'=2,'wa_1'=4,'wa_2'=8,'ba'=4] {'wa_1'}, use_global_device_ids=true, to_apply=%region_7.8 | all-reduce | flops 4096 | bytes 32768 | tf_op jit(solution)/shard_map/psum | solution.py:20
  164.5 32.8 %psum.47 = f32[4,8,128]{2,0,1:T(4,128)S(1)} all-reduce(f32[4,8,128]{2,0,1:T(4,128)S(1)} %psum.46), channel_id=1, replica_groups=mesh['wa_0'=2,'wa_1'=4,'wa_2'=8,'ba'=4] {'wa_2'}, use_global_device_ids=true, to_apply=%region_8.9 | all-reduce | flops 4096 | bytes 32768 | tf_op jit(solution)/shard_map/psum | solution.py:20
  197.3 1.1 divide_multiply_fusion
  198.5 1.3 fusion.120
  200.4 1.6 convolution_convert_fusion
  202.1 5.1 %fusion.115 = bf16[2,36,1024]{2,1,0:T(8,128)(2,1)S(1)} fusion(bf16[2,1024,320]{1,2,0:T(8,128)(2,1)} %convolution_convert_fusion, f32[2,1024,320]{1,2,0:T(8,128)S(1)} %fusion.187, f32[2,1024,320]{1,2,0:T(8,128)} %copy-done.16, f32[320]{0:T(512)S(1)} %copy-done.11, bf16[320,320]{1,0:T(8,128)(2,1)S(1)} %copy-done, bf16[320,36]{0,1:T(8,128)(2,1)S(1)} %copy-done.2), kind=kOutput, calls=%fused_computation.119 | convolution fusion | flops 482418688 | bytes 6930176 | tf_op jit(solution)/shard_map/transpose(jvp(vmap()))/dot_general | solution.py:66
  207.5 0.7 multiply_reduce_fusion
  208.8 15.8 %all_to_all.12 = f32[64,1,1]{2,1,0:T(1,128)S(1)} all-to-all(f32[64,1,1]{2,1,0:T(1,128)S(1)} %broadcast_in_dim.11), channel_id=1, replica_groups=mesh['wa_0'=2,'wa_1'=4,'wa_2'=8,'ba'=4] {'wa_0','wa_1','wa_2'}, dimensions={0} | all-to-all | bytes 512 | tf_op jit(solution)/shard_map/all_to_all | solution.py:26
  224.6 0.7 reduce_sum.49
  225.9 1.3 dynamic_update_slice.14
  227.3 1.3 dynamic_update_slice.15
  228.6 0.7 collective-permute-start.4
  229.4 8.8 %collective-permute-done.4 = f32[4,8,128]{2,0,1:T(4,128)S(1)} collective-permute-done((f32[4,8,128]{2,0,1:T(4,128)S(1)}, f32[4,8,128]{2,0,1:T(4,128)S(1)}, u32[]{:S(2)}, u32[]{:S(2)}) %collective-permute-start.4) | collective-permute-done | bytes 16416 | tf_op jit(solution)/shard_map/ppermute | solution.py:35
  238.2 0.6 copy.97
  (108 shorter events, 6.3 us)
Async XLA Ops:
  0.0 24.1 %copy-start = (bf16[320,320]{1,0:T(8,128)(2,1)S(1)}, bf16[320,320]{1,0:T(8,128)(2,1)}, u32[]{:S(2)}) copy-start(bf16[320,320]{1,0:T(8,128)(2,1)} %param.16) | copy-start | bytes 614404
  0.8 21.1 %collective-permute-start = (f32[4,8,128]{2,0,1:T(4,128)S(1)}, f32[4,8,128]{2,0,1:T(4,128)S(1)}, u32[]{:S(2)}, u32[]{:S(2)}) collective-permute-start(f32[4,8,128]{2,0,1:T(4,128)S(1)} %get-tuple-element.43), channel_id=1, source_target_pairs={{0,252},{4,0},{8,4},{12,8},{16,12},{20,16},{24,20},{28,24},{32,28}... | collective-permute-start | bytes 49160 | tf_op jit(solution)/shard_map/ppermute | solution.py:35
  11.4 1.2 copy-start.14
  12.0 110.0 %collective-permute-start.2 = (f32[128]{0:T(128)}, f32[128]{0:T(128)}, u32[]{:S(2)}, u32[]{:S(2)}) collective-permute-start(f32[128]{0:T(128)} %slice.200), channel_id=1, source_target_pairs={{0,4},{4,8},{8,12},{12,16},{16,20},{20,24},{24,28},{28,32},{32,36}... | collective-permute-start | bytes 1544 | tf_op jit(solution)/shard_map/ppermute | solution.py:35
  13.9 12.7 %copy-start.12 = (f32[320]{0:T(512)}, f32[320]{0:T(512)S(1)}, u32[]{:S(2)}) copy-start(f32[320]{0:T(512)S(1)} %get-tuple-element.6) | copy-start | bytes 3844
  24.1 2.6 %copy-start.3 = (bf16[36,320]{1,0:T(8,128)(2,1)S(1)}, bf16[36,320]{1,0:T(8,128)(2,1)}, u32[]{:S(2)}) copy-start(bf16[36,320]{1,0:T(8,128)(2,1)} %param.17) | copy-start | bytes 69124
  29.4 60.8 %copy-start.7 = (f32[64,4]{0,1:T(4,128)S(1)}, f32[64,4]{0,1:T(4,128)}, u32[]{:S(2)}) copy-start(f32[64,4]{0,1:T(4,128)} %param.19) | copy-start | bytes 3076
  90.2 2.9 %copy-start.1 = (bf16[320,36]{0,1:T(8,128)(2,1)S(1)}, bf16[320,36]{0,1:T(8,128)(2,1)}, u32[]{:S(2)}) copy-start(bf16[320,36]{0,1:T(8,128)(2,1)} %param.15) | copy-start | bytes 69124
  90.2 2.8 %copy-start.13 = (f32[320]{0:T(512)S(1)}, f32[320]{0:T(512)}, u32[]{:S(2)}) copy-start(f32[320]{0:T(512)} %copy-done.12) | copy-start | bytes 3844
  93.0 12.2 %copy-start.6 = (f32[2,4,8,128]{3,2,1,0:T(8,128)S(1)}, f32[2,4,8,128]{3,2,1,0:T(8,128)}, u32[]{:S(2)}) copy-start(f32[2,4,8,128]{3,2,1,0:T(8,128)} %param.11) | copy-start | bytes 98308
  93.0 28.9 %copy-start.15 = (f32[256]{0:T(256)S(1)}, f32[256]{0:T(256)}, u32[]{:S(2)}) copy-start(f32[256]{0:T(256)} %copy-done.14) | copy-start | bytes 3076
  98.3 37.9 %copy-start.10 = (f32[320]{0:T(512)S(1)}, f32[320]{0:T(512)}, u32[]{:S(2)}) copy-start(f32[320]{0:T(512)} %get-tuple-element.5) | copy-start | bytes 3844
  100.4 16.6 %all-to-all-start = ((f32[64,1,1]{2,1,0:T(1,128)}), f32[64,1,1]{2,1,0:T(1,128)S(1)}, u32[]{:S(2)}, u32[]{:S(2)}) async-start(f32[64,1,1]{2,1,0:T(1,128)} %broadcast_in_dim.9), calls=%async_computation | async-start | bytes 65536 | tf_op jit(solution)/shard_map/all_to_all | solution.py:26
  121.2 9.5 %collective-permute-start.1 = (f32[4,8,128]{2,0,1:T(4,128)S(1)}, f32[4,8,128]{2,0,1:T(4,128)S(1)}, u32[]{:S(2)}, u32[]{:S(2)}) collective-permute-start(f32[4,8,128]{2,0,1:T(4,128)S(1)} %slice.230), channel_id=1, source_target_pairs={{0,4},{4,8},{8,12},{12,16},{16,20},{20,24},{24,28},{28,32},{32,36}... | collective-permute-start | bytes 49160 | tf_op jit(solution)/shard_map/ppermute | solution.py:35
  122.5 10.9 %copy-start.8 = (f32[128]{0:T(128)}, f32[128]{0:T(128)S(1)}, u32[]{:S(2)}) copy-start(f32[128]{0:T(128)S(1)} %slice_add_fusion.2) | copy-start | bytes 1540
  130.8 3.8 %collective-permute-start.3 = (f32[4,8,128]{2,0,1:T(4,128)S(1)}, f32[4,8,128]{2,0,1:T(4,128)S(1)}, u32[]{:S(2)}, u32[]{:S(2)}) collective-permute-start(f32[4,8,128]{2,0,1:T(4,128)S(1)} %divide_add_fusion.1), channel_id=1, source_target_pairs={{0,252},{4,0},{8,4},{12,8},{16,12},{20,16},{24,20},{28,24},{32,28}... | collective-permute-start | bytes 49160 | tf_op jit(solution)/shard_map/ppermute | solution.py:35
  137.2 1.5 copy-start.16
  198.5 1.9 copy-start.4
  198.5 3.6 %copy-start.2 = (bf16[320,36]{0,1:T(8,128)(2,1)S(1)}, bf16[320,36]{0,1:T(8,128)(2,1)}, u32[]{:S(2)}) copy-start(bf16[320,36]{0,1:T(8,128)(2,1)} %param.15) | copy-start | bytes 69124
  199.8 2.2 copy-start.11
  202.0 36.1 %copy-start.5 = (f32[1,4,8,128]{3,2,1,0:T(8,128)S(1)}, f32[1,4,8,128]{3,2,1,0:T(8,128)}, u32[]{:S(2)}) copy-start(f32[1,4,8,128]{3,2,1,0:T(8,128)} %get-tuple-element.42) | copy-start | bytes 49156
  202.0 36.1 %copy-start.9 = (f32[128]{0:T(128)S(1)}, f32[128]{0:T(128)}, u32[]{:S(2)}) copy-start(f32[128]{0:T(128)} %copy-done.8) | copy-start | bytes 1540
  228.6 9.5 %collective-permute-start.4 = (f32[4,8,128]{2,0,1:T(4,128)S(1)}, f32[4,8,128]{2,0,1:T(4,128)S(1)}, u32[]{:S(2)}, u32[]{:S(2)}) collective-permute-start(f32[4,8,128]{2,0,1:T(4,128)S(1)} %slice.235), channel_id=1, source_target_pairs={{0,4},{4,8},{8,12},{12,16},{16,20},{20,24},{24,28},{28,32},{32,36}... | collective-permute-start | bytes 49160 | tf_op jit(solution)/shard_map/ppermute | solution.py:35
where the time goes:
time: 240 us; the launch traced here: 239 us
  blocking collectives  130 us (54%)
  matrix products  29.2 us (12%)
  waiting for transfers between devices  28.9 us (12%)
  local copies, waits for them, and re-layouts  16.4 us (7%)
  starting transfers between devices  16.1 us (7%)
  between operations  11.6 us (5%)
  other arithmetic  6.67 us (3%)
    psum x6, blocking collectives, broadcast_by_axis(): shard = lax.psum(shard, axis)  114 us
    ppermute x5, waiting for transfers between devices, passed_along(): lax.ppermute(shard, axis, [(i, (i + by) % length) for i in range(length)])  18.3 us
    all_to_all x1, blocking collectives, from_everyone(): return lax.all_to_all(copies, axis, split_axis=0, concat_axis=0, tiled=True)  15.8 us
    dot_general x4, matrix products, denoise(): jnp.dot(w_in, stacked, preferred_element_type=jnp.float32)  12 us
    ppermute x5, starting transfers between devices, passed_along(): lax.ppermute(shard, axis, [(i, (i + by) % length) for i in range(length)])  11.3 us
    all_to_all x1, waiting for transfers between devices, from_everyone(): return lax.all_to_all(copies, axis, split_axis=0, concat_axis=0, tiled=True)  10.6 us
    dot_general x6, matrix products, percept(): jnp.einsum('fc,chw->fhw', w_feat, cleaned, precision=lax.Precision.HIGHEST)  6.83 us
    dot_general x4, matrix products, denoise(): jnp.dot(w_out, joined, preferred_element_type=jnp.float32)  6.8 us
  transfers between devices with their start and end apart: 6, of which 4 were waited for; matrix products, arithmetic and copies ran while one was open for 12% of the time, Pallas kernels for 0%

commit v1 on v0

--- a/solution.py
+++ b/solution.py
@@ -17,7 +17,8 @@
 def broadcast_by_axis(shard, axes, root):
     shard = jnp.where(lax.axis_index(axes) == root, shard, jnp.zeros_like(shard))
     for axis in axes:
-        shard = lax.psum(shard, axis)
+        parts = lax.all_gather(shard, axis, axis=0, tiled=False)
+        shard = parts.sum(axis=0)
     return shard
 
 

time: 240 us -> 220 us (0.917)
  blocking collectives: 130 us -> 105 us
  starting transfers between devices: 16.1 us -> 21.3 us
    psum x6 -> x0, blocking collectives: 114 us -> none  [broadcast_by_axis(): shard = lax.psum(shard, axis)]
    all_gather x0 -> x6, blocking collectives: none -> 85 us  [broadcast_by_axis(): parts = lax.all_gather(shard, axis, axis=0, tiled=False)]
    all_to_all x1, starting transfers between devices: 4.77 us -> 9.81 us  [from_everyone(): return lax.all_to_all(copies, axis, split_axis=0, concat_axis=0, tiled=True)]
    all_to_all x1, blocking collectives: 15.8 us -> 19.7 us  [from_everyone(): return lax.all_to_all(copies, axis, split_axis=0, concat_axis=0, tiled=True)]
    unnamed x49 -> x71, local copies, waits for them, and re-layouts: 3.3 us -> 4.85 us
  transfers between devices with their start and end apart: 6 -> 6, of which waited for: 4 -> 4; matrix products, arithmetic and copies ran while one was open for 12% -> 13% of each run, Pallas kernels for 0% -> 0%
where the time goes in v1:
time: 220 us; the launch traced here: 219 us
  blocking collectives  105 us (48%)
  waiting for transfers between devices  29.1 us (13%)
  matrix products  26.8 us (12%)
  starting transfers between devices  21.3 us (10%)
  local copies, waits for them, and re-layouts  17.9 us (8%)
  between operations  11.5 us (5%)
  other arithmetic  7.99 us (4%)
    all_gather x6, blocking collectives, broadcast_by_axis(): parts = lax.all_gather(shard, axis, axis=0, tiled=False)  85 us
    all_to_all x1, blocking collectives, from_everyone(): return lax.all_to_all(copies, axis, split_axis=0, concat_axis=0, tiled=True)  19.7 us
    ppermute x5, waiting for transfers between devices, passed_along(): lax.ppermute(shard, axis, [(i, (i + by) % length) for i in range(length)])  18.3 us
    dot_general x4, matrix products, denoise(): jnp.dot(w_in, stacked, preferred_element_type=jnp.float32)  12 us
    ppermute x5, starting transfers between devices, passed_along(): lax.ppermute(shard, axis, [(i, (i + by) % length) for i in range(length)])  11.5 us
    all_to_all x1, waiting for transfers between devices, from_everyone(): return lax.all_to_all(copies, axis, split_axis=0, concat_axis=0, tiled=True)  10.7 us
    all_to_all x1, starting transfers between devices, from_everyone(): return lax.all_to_all(copies, axis, split_axis=0, concat_axis=0, tiled=True)  9.81 us
    dot_general x4, matrix products, denoise(): jnp.dot(w_out, joined, preferred_element_type=jnp.float32)  6.55 us
  transfers between devices with their start and end apart: 6, of which 4 were waited for; matrix products, arithmetic and copies ran while one was open for 13% of the time, Pallas kernels for 0%

profile of v1, /device:TPU:2, one launch (start us, length us, event | category | flops | bytes accessed | tf_op | source)
XLA Modules:
  0.0 219.4 jit_solution(18068420607774785316)
XLA Ops:
  0.0 0.8 fusion.241
  0.8 9.9 %collective-permute-start = (f32[4,8,128]{2,0,1:T(4,128)S(1)}, f32[4,8,128]{2,0,1:T(4,128)S(1)}, u32[]{:S(2)}, u32[]{:S(2)}) collective-permute-start(f32[4,8,128]{2,0,1:T(4,128)S(1)} %get-tuple-element.43), channel_id=1, source_target_pairs={{0,252},{4,0},{8,4},{12,8},{16,12},{20,16},{24,20},{28,24},{32,28}... | collective-permute-start | bytes 49160 | tf_op jit(solution)/shard_map/ppermute | solution.py:36
  10.6 0.7 broadcast_add_fusion
  12.5 1.3 slice_reduce_fusion
  13.9 1.3 fusion.242
  22.4 1.3 fusion.190
  23.7 1.0 fusion.88
  24.8 1.5 copy-done.26
  26.3 0.9 fusion.94
  27.4 0.8 fusion.180
  28.2 5.9 %all_gather.32 = f32[2,4,8,128]{3,2,1,0:T(8,128)S(1)} all-gather(f32[1,4,8,128]{3,2,1,0:T(8,128)S(1)} %copy.150), channel_id=1, replica_groups=mesh['wa_0'=2,'wa_1'=4,'wa_2'=8,'ba'=4] {'wa_0'}, dimensions={0}, use_global_device_ids=true | all-gather | bytes 49152 | tf_op jit(solution)/shard_map/all_gather | solution.py:20
  34.1 11.9 %all-gather = f32[16,8,128]{2,1,0:T(8,128)S(1)} all-gather(f32[4,8,128]{2,1,0:T(8,128)S(1)} %reduce_sum.99), channel_id=2, replica_groups=mesh['wa_0'=2,'wa_1'=4,'wa_2'=8,'ba'=4] {'wa_1'}, dimensions={0}, use_global_device_ids=true | all-gather | bytes 81920 | tf_op jit(solution)/shard_map/all_gather | solution.py:20
  45.9 24.9 %all-gather.1 = f32[32,8,128]{2,1,0:T(8,128)S(1)} all-gather(f32[4,8,128]{2,1,0:T(8,128)S(1)} %reduce_sum.100), channel_id=3, replica_groups=mesh['wa_0'=2,'wa_1'=4,'wa_2'=8,'ba'=4] {'wa_2'}, dimensions={0}, use_global_device_ids=true | all-gather | bytes 147456 | tf_op jit(solution)/shard_map/all_gather | solution.py:20
  70.8 1.3 convolution_bitcast_fusion.1
  72.1 1.1 divide_multiply_fusion.1
  73.3 1.3 fusion.121
  75.2 2.4 %convolution_convert_fusion.1 = bf16[2,1024,320]{1,2,0:T(8,128)(2,1)} fusion(bf16[2,36,1024]{2,1,0:T(8,128)(2,1)S(1)} %reshape.151, bf16[36,320]{1,0:T(8,128)(2,1)} %param.17), kind=kOutput, calls=%fused_computation.101 | convolution fusion | flops 47185920 | bytes 1481216 | tf_op jit(solution)/shard_map/transpose(jvp(vmap()))/dot_general | solution.py:71
  77.6 5.1 %fusion.110 = bf16[2,36,1024]{2,1,0:T(8,128)(2,1)S(1)} fusion(bf16[2,1024,320]{1,2,0:T(8,128)(2,1)} %convolution_convert_fusion.1, f32[2,1024,320]{1,2,0:T(8,128)S(1)} %fusion.190, f32[2,1024,320]{1,2,0:T(8,128)} %copy-done.26, f32[320]{0:T(512)S(1)} %copy-done.23, bf16[320,320]{1,0:T(8,128)(2,1)S(1)} %copy-done, bf16[320,36]{0,1:T(8,128)(2,1)S(1)} %copy-done.11), kind=kOutput, calls=%fused_computation.118 | convolution fusion | flops 482418688 | bytes 6930176 | tf_op jit(solution)/shard_map/transpose(jvp(vmap()))/dot_general | solution.py:67
  83.0 0.7 multiply_reduce_fusion.1
  83.8 1.3 broadcast_in_dim.9
  85.0 9.8 %all-to-all-start = ((f32[64,1,1]{2,1,0:T(1,128)}), f32[64,1,1]{2,1,0:T(1,128)S(1)}, u32[]{:S(2)}, u32[]{:S(2)}) async-start(f32[64,1,1]{2,1,0:T(1,128)} %broadcast_in_dim.9), calls=%async_computation | async-start | bytes 65536 | tf_op jit(solution)/shard_map/all_to_all | solution.py:27
  94.9 0.6 slice_multiply_fusion.1
  96.1 10.7 %all-to-all-done = f32[64,1,1]{2,1,0:T(1,128)S(1)} async-done(((f32[64,1,1]{2,1,0:T(1,128)}), f32[64,1,1]{2,1,0:T(1,128)S(1)}, u32[]{:S(2)}, u32[]{:S(2)}) %all-to-all-start) | async-done | bytes 288 | tf_op jit(solution)/shard_map/all_to_all | solution.py:27
  106.9 0.7 reduce_sum.103
  108.3 1.3 dynamic_update_slice.12
  109.8 1.3 dynamic_update_slice.13
  111.1 0.9 collective-permute-start.1
  112.5 8.3 %collective-permute-done.1 = f32[4,8,128]{2,0,1:T(4,128)S(1)} collective-permute-done((f32[4,8,128]{2,0,1:T(4,128)S(1)}, f32[4,8,128]{2,0,1:T(4,128)S(1)}, u32[]{:S(2)}, u32[]{:S(2)}) %collective-permute-start.1) | collective-permute-done | bytes 16416 | tf_op jit(solution)/shard_map/ppermute | solution.py:36
  123.4 1.3 collective-permute-done.3
  126.2 1.0 fusion.86
  127.3 1.5 copy-done.27
  128.8 0.9 fusion.97
  129.9 0.8 fusion.178
  130.6 0.6 convolution_bitcast_fusion
  131.3 5.9 %all_gather.37 = f32[2,4,8,128]{3,2,1,0:T(8,128)S(1)} all-gather(f32[1,4,8,128]{3,2,1,0:T(8,128)S(1)} %copy.166), channel_id=1, replica_groups=mesh['wa_0'=2,'wa_1'=4,'wa_2'=8,'ba'=4] {'wa_0'}, dimensions={0}, use_global_device_ids=true | all-gather | bytes 49152 | tf_op jit(solution)/shard_map/all_gather | solution.py:20
  137.2 11.9 %all-gather.2 = f32[16,8,128]{2,1,0:T(8,128)S(1)} all-gather(f32[4,8,128]{2,1,0:T(8,128)S(1)} %reduce_sum.105), channel_id=4, replica_groups=mesh['wa_0'=2,'wa_1'=4,'wa_2'=8,'ba'=4] {'wa_1'}, dimensions={0}, use_global_device_ids=true | all-gather | bytes 81920 | tf_op jit(solution)/shard_map/all_gather | solution.py:20
  149.1 24.6 %all-gather.3 = f32[32,8,128]{2,1,0:T(8,128)S(1)} all-gather(f32[4,8,128]{2,1,0:T(8,128)S(1)} %reduce_sum.106), channel_id=5, replica_groups=mesh['wa_0'=2,'wa_1'=4,'wa_2'=8,'ba'=4] {'wa_2'}, dimensions={0}, use_global_device_ids=true | all-gather | bytes 147456 | tf_op jit(solution)/shard_map/all_gather | solution.py:20
  174.2 1.3 fusion.120
  176.1 2.4 %convolution_convert_fusion = bf16[2,1024,320]{1,2,0:T(8,128)(2,1)} fusion(bf16[2,36,1024]{2,1,0:T(8,128)(2,1)S(1)} %reshape.155, bf16[36,320]{1,0:T(8,128)(2,1)} %param.17), kind=kOutput, calls=%fused_computation.100 | convolution fusion | flops 47185920 | bytes 1481216 | tf_op jit(solution)/shard_map/transpose(jvp(vmap()))/dot_general | solution.py:71
  178.5 5.1 %fusion.115 = bf16[2,36,1024]{2,1,0:T(8,128)(2,1)S(1)} fusion(bf16[2,1024,320]{1,2,0:T(8,128)(2,1)} %convolution_convert_fusion, f32[2,1024,320]{1,2,0:T(8,128)S(1)} %fusion.187, f32[2,1024,320]{1,2,0:T(8,128)} %copy-done.27, f32[320]{0:T(512)S(1)} %copy-done.21, bf16[320,320]{1,0:T(8,128)(2,1)S(1)} %copy-done, bf16[320,36]{0,1:T(8,128)(2,1)S(1)} %copy-done.12), kind=kOutput, calls=%fused_computation.119 | convolution fusion | flops 482418688 | bytes 6930176 | tf_op jit(solution)/shard_map/transpose(jvp(vmap()))/dot_general | solution.py:67
  183.9 0.7 multiply_reduce_fusion
  184.6 0.6 broadcast_in_dim.11
  185.3 19.7 %all_to_all.12 = f32[64,1,1]{2,1,0:T(1,128)S(1)} all-to-all(f32[64,1,1]{2,1,0:T(1,128)S(1)} %broadcast_in_dim.11), channel_id=1, replica_groups=mesh['wa_0'=2,'wa_1'=4,'wa_2'=8,'ba'=4] {'wa_0','wa_1','wa_2'}, dimensions={0} | all-to-all | bytes 512 | tf_op jit(solution)/shard_map/all_to_all | solution.py:27
  205.0 0.7 reduce_sum.109
  206.5 1.3 dynamic_update_slice.14
  207.9 1.3 dynamic_update_slice.15
  209.2 0.7 collective-permute-start.4
  209.9 8.8 %collective-permute-done.4 = f32[4,8,128]{2,0,1:T(4,128)S(1)} collective-permute-done((f32[4,8,128]{2,0,1:T(4,128)S(1)}, f32[4,8,128]{2,0,1:T(4,128)S(1)}, u32[]{:S(2)}, u32[]{:S(2)}) %collective-permute-start.4) | collective-permute-done | bytes 16416 | tf_op jit(solution)/shard_map/ppermute | solution.py:36
  (138 shorter events, 7.7 us)
Async XLA Ops:
  0.0 23.7 %copy-start = (bf16[320,320]{1,0:T(8,128)(2,1)S(1)}, bf16[320,320]{1,0:T(8,128)(2,1)}, u32[]{:S(2)}) copy-start(bf16[320,320]{1,0:T(8,128)(2,1)} %param.16) | copy-start | bytes 614404
  0.8 20.7 %collective-permute-start = (f32[4,8,128]{2,0,1:T(4,128)S(1)}, f32[4,8,128]{2,0,1:T(4,128)S(1)}, u32[]{:S(2)}, u32[]{:S(2)}) collective-permute-start(f32[4,8,128]{2,0,1:T(4,128)S(1)} %get-tuple-element.43), channel_id=1, source_target_pairs={{0,252},{4,0},{8,4},{12,8},{16,12},{20,16},{24,20},{28,24},{32,28}... | collective-permute-start | bytes 49160 | tf_op jit(solution)/shard_map/ppermute | solution.py:36
  11.4 1.1 copy-start.24
  11.9 100.0 %collective-permute-start.2 = (f32[128]{0:T(128)}, f32[128]{0:T(128)}, u32[]{:S(2)}, u32[]{:S(2)}) collective-permute-start(f32[128]{0:T(128)} %slice.200), channel_id=1, source_target_pairs={{0,4},{4,8},{8,12},{12,16},{16,20},{20,24},{24,28},{28,32},{32,36}... | collective-permute-start | bytes 1544 | tf_op jit(solution)/shard_map/ppermute | solution.py:36
  13.9 10.9 %copy-start.22 = (f32[320]{0:T(512)}, f32[320]{0:T(512)S(1)}, u32[]{:S(2)}) copy-start(f32[320]{0:T(512)S(1)} %get-tuple-element.6) | copy-start | bytes 3844
  21.5 5.8 %copy-start.1 = (f32[1,4,8,128]{3,1,2,0:T(4,128)}, f32[1,4,8,128]{3,1,2,0:T(4,128)S(1)}, u32[]{:S(2)}) copy-start(f32[1,4,8,128]{3,1,2,0:T(4,128)S(1)} %get-tuple-element.39) | copy-start | bytes 49156
  21.5 5.8 %copy-start.3 = (f32[1,4,8,128]{3,1,2,0:T(4,128)}, f32[1,4,8,128]{3,1,2,0:T(4,128)S(1)}, u32[]{:S(2)}) copy-start(f32[1,4,8,128]{3,1,2,0:T(4,128)S(1)} %get-tuple-element.40) | copy-start | bytes 49156
  23.7 2.6 %copy-start.13 = (bf16[36,320]{1,0:T(8,128)(2,1)S(1)}, bf16[36,320]{1,0:T(8,128)(2,1)}, u32[]{:S(2)}) copy-start(bf16[36,320]{1,0:T(8,128)(2,1)} %param.17) | copy-start | bytes 69124
  24.8 1.5 copy-start.26
  74.6 2.9 %copy-start.11 = (bf16[320,36]{0,1:T(8,128)(2,1)S(1)}, bf16[320,36]{0,1:T(8,128)(2,1)}, u32[]{:S(2)}) copy-start(bf16[320,36]{0,1:T(8,128)(2,1)} %param.15) | copy-start | bytes 69124
  74.6 2.9 %copy-start.23 = (f32[320]{0:T(512)S(1)}, f32[320]{0:T(512)}, u32[]{:S(2)}) copy-start(f32[320]{0:T(512)} %copy-done.22) | copy-start | bytes 3844
  77.6 17.3 %copy-start.16 = (f32[2,4,8,128]{3,2,1,0:T(8,128)S(1)}, f32[2,4,8,128]{3,2,1,0:T(8,128)}, u32[]{:S(2)}) copy-start(f32[2,4,8,128]{3,2,1,0:T(8,128)} %param.11) | copy-start | bytes 98308
  77.6 30.7 %copy-start.2 = (f32[1,4,8,128]{3,1,2,0:T(4,128)S(1)}, f32[1,4,8,128]{3,1,2,0:T(4,128)}, u32[]{:S(2)}) copy-start(f32[1,4,8,128]{3,1,2,0:T(4,128)} %copy-done.1) | copy-start | bytes 49156
  77.6 30.7 %copy-start.4 = (f32[1,4,8,128]{3,1,2,0:T(4,128)S(1)}, f32[1,4,8,128]{3,1,2,0:T(4,128)}, u32[]{:S(2)}) copy-start(f32[1,4,8,128]{3,1,2,0:T(4,128)} %copy-done.3) | copy-start | bytes 49156
  77.6 30.7 %copy-start.9 = (f32[2,1,4,8,128]{4,2,3,0,1:T(4,128)S(1)}, f32[2,1,4,8,128]{4,2,3,0,1:T(4,128)}, u32[]{:S(2)}) copy-start(f32[2,1,4,8,128]{4,2,3,0,1:T(4,128)} %get-tuple-element.14) | copy-start | bytes 98308
  77.6 34.4 %copy-start.25 = (f32[256]{0:T(256)S(1)}, f32[256]{0:T(256)}, u32[]{:S(2)}) copy-start(f32[256]{0:T(256)} %copy-done.24) | copy-start | bytes 3076
  82.8 43.3 %copy-start.20 = (f32[320]{0:T(512)S(1)}, f32[320]{0:T(512)}, u32[]{:S(2)}) copy-start(f32[320]{0:T(512)} %get-tuple-element.5) | copy-start | bytes 3844
  85.0 21.8 %all-to-all-start = ((f32[64,1,1]{2,1,0:T(1,128)}), f32[64,1,1]{2,1,0:T(1,128)S(1)}, u32[]{:S(2)}, u32[]{:S(2)}) async-start(f32[64,1,1]{2,1,0:T(1,128)} %broadcast_in_dim.9), calls=%async_computation | async-start | bytes 65536 | tf_op jit(solution)/shard_map/all_to_all | solution.py:27
  111.1 9.7 %collective-permute-start.1 = (f32[4,8,128]{2,0,1:T(4,128)S(1)}, f32[4,8,128]{2,0,1:T(4,128)S(1)}, u32[]{:S(2)}, u32[]{:S(2)}) collective-permute-start(f32[4,8,128]{2,0,1:T(4,128)S(1)} %slice.230), channel_id=1, source_target_pairs={{0,4},{4,8},{8,12},{12,16},{16,20},{20,24},{24,28},{28,32},{32,36}... | collective-permute-start | bytes 49160 | tf_op jit(solution)/shard_map/ppermute | solution.py:36
  112.5 13.6 %copy-start.18 = (f32[128]{0:T(128)}, f32[128]{0:T(128)S(1)}, u32[]{:S(2)}) copy-start(f32[128]{0:T(128)S(1)} %slice_add_fusion.2) | copy-start | bytes 1540
  120.8 3.8 %collective-permute-start.3 = (f32[4,8,128]{2,0,1:T(4,128)S(1)}, f32[4,8,128]{2,0,1:T(4,128)S(1)}, u32[]{:S(2)}, u32[]{:S(2)}) collective-permute-start(f32[4,8,128]{2,0,1:T(4,128)S(1)} %divide_add_fusion.1), channel_id=1, source_target_pairs={{0,252},{4,0},{8,4},{12,8},{16,12},{20,16},{24,20},{28,24},{32,28}... | collective-permute-start | bytes 49160 | tf_op jit(solution)/shard_map/ppermute | solution.py:36
  124.7 5.1 %copy-start.5 = (f32[1,4,8,128]{3,1,2,0:T(4,128)}, f32[1,4,8,128]{3,1,2,0:T(4,128)S(1)}, u32[]{:S(2)}) copy-start(f32[1,4,8,128]{3,1,2,0:T(4,128)S(1)} %get-tuple-element.35) | copy-start | bytes 49156
  124.8 5.1 %copy-start.7 = (f32[1,4,8,128]{3,1,2,0:T(4,128)}, f32[1,4,8,128]{3,1,2,0:T(4,128)S(1)}, u32[]{:S(2)}) copy-start(f32[1,4,8,128]{3,1,2,0:T(4,128)S(1)} %get-tuple-element.36) | copy-start | bytes 49156
  126.2 2.6 %copy-start.14 = (bf16[36,320]{1,0:T(8,128)(2,1)S(1)}, bf16[36,320]{1,0:T(8,128)(2,1)}, u32[]{:S(2)}) copy-start(bf16[36,320]{1,0:T(8,128)(2,1)} %param.17) | copy-start | bytes 69124
  127.3 1.5 copy-start.27
  128.8 1.9 copy-start.17
  175.5 2.9 %copy-start.12 = (bf16[320,36]{0,1:T(8,128)(2,1)S(1)}, bf16[320,36]{0,1:T(8,128)(2,1)}, u32[]{:S(2)}) copy-start(bf16[320,36]{0,1:T(8,128)(2,1)} %param.15) | copy-start | bytes 69124
  175.5 2.9 %copy-start.21 = (f32[320]{0:T(512)S(1)}, f32[320]{0:T(512)}, u32[]{:S(2)}) copy-start(f32[320]{0:T(512)} %get-tuple-element.5) | copy-start | bytes 3844
  178.4 28.0 %copy-start.6 = (f32[1,4,8,128]{3,1,2,0:T(4,128)S(1)}, f32[1,4,8,128]{3,1,2,0:T(4,128)}, u32[]{:S(2)}) copy-start(f32[1,4,8,128]{3,1,2,0:T(4,128)} %copy-done.5) | copy-start | bytes 49156
  178.4 28.0 %copy-start.8 = (f32[1,4,8,128]{3,1,2,0:T(4,128)S(1)}, f32[1,4,8,128]{3,1,2,0:T(4,128)}, u32[]{:S(2)}) copy-start(f32[1,4,8,128]{3,1,2,0:T(4,128)} %copy-done.7) | copy-start | bytes 49156
  178.4 28.0 %copy-start.10 = (f32[2,1,4,8,128]{4,2,3,0,1:T(4,128)S(1)}, f32[2,1,4,8,128]{4,2,3,0,1:T(4,128)}, u32[]{:S(2)}) copy-start(f32[2,1,4,8,128]{4,2,3,0,1:T(4,128)} %get-tuple-element.10) | copy-start | bytes 98308
  178.4 40.3 %copy-start.15 = (f32[1,4,8,128]{3,2,1,0:T(8,128)S(1)}, f32[1,4,8,128]{3,2,1,0:T(8,128)}, u32[]{:S(2)}) copy-start(f32[1,4,8,128]{3,2,1,0:T(8,128)} %get-tuple-element.42) | copy-start | bytes 49156
  178.5 40.3 %copy-start.19 = (f32[128]{0:T(128)S(1)}, f32[128]{0:T(128)}, u32[]{:S(2)}) copy-start(f32[128]{0:T(128)} %copy-done.18) | copy-start | bytes 1540
  209.2 9.5 %collective-permute-start.4 = (f32[4,8,128]{2,0,1:T(4,128)S(1)}, f32[4,8,128]{2,0,1:T(4,128)S(1)}, u32[]{:S(2)}, u32[]{:S(2)}) collective-permute-start(f32[4,8,128]{2,0,1:T(4,128)S(1)} %slice.235), channel_id=1, source_target_pairs={{0,4},{4,8},{8,12},{12,16},{16,20},{20,24},{24,28},{28,32},{32,36}... | collective-permute-start | bytes 49160 | tf_op jit(solution)/shard_map/ppermute | solution.py:36
